TPU v7x, 256 devices: a whole 4x4x8 slice. The times are simulated.
256 devices in a mesh: dp: 128 (over y, x_hi, z, core), mp: 2 (over x_lo).
Axes of the slice: x: 4 (x_hi: 2, x_lo: 2; x = x_hi * 2 + x_lo), y: 4, z: 8, core: 2. Of those that a mesh axis runs over, the one named last changes fastest.
Arguments:
- dino_tokens: bfloat16 [65536, 1024], P('dp', 'mp'), may hold values from -6 to 6
- siglip_tokens: bfloat16 [65536, 1152], P('dp', 'mp'), may hold values from -6 to 6
- dino_norm_one: float32 [1024], replicated, may hold values from 0.25 to 1.75
- dino_qkv: bfloat16 [1024, 3, 1024], P('dp', None, 'mp'), may hold values from -6.05625 to 6.05625
- dino_out: bfloat16 [1024, 1024], P('mp', 'dp'), may hold values from -0.1875 to 0.1875
- dino_norm_two: float32 [1024], replicated, may hold values from 0.25 to 1.75
- dino_up: bfloat16 [1024, 4096], P('dp', 'mp'), may hold values from -0.1875 to 0.1875
- dino_down: bfloat16 [4096, 1024], P('mp', 'dp'), may hold values from -0.09375 to 0.09375
- siglip_norm_one: float32 [1152], replicated, may hold values from 0.25 to 1.75
- siglip_qkv: bfloat16 [1152, 3, 1152], P('dp', None, 'mp'), may hold values from -5.709887 to 5.709887
- siglip_out: bfloat16 [1152, 1152], P('mp', 'dp'), may hold values from -0.1875 to 0.1875
- siglip_norm_two: float32 [1152], replicated, may hold values from 0.25 to 1.75
- siglip_up: bfloat16 [1152, 4304], P('dp', 'mp'), may hold values from -0.1875 to 0.1875
- siglip_down: bfloat16 [4304, 1152], P('mp', 'dp'), may hold values from -0.09375 to 0.09375
Outputs:
- dino_result: bfloat16 [65536, 1024], P('dp', 'mp')
- siglip_result: bfloat16 [65536, 1152], P('dp', 'mp')
All inputs are finite; a program needn't handle non-finite values.
Results may differ from a plain program's by a relative error of at most 0.012.
Values may be sent and summed in bfloat16 or wider, within the bound.
A program may use at most 128 MiB of HBM per device.

v0:
```python
import math
import jax
import jax.numpy as jnp
from jax import lax
from jax.sharding import PartitionSpec as P

HEADS = 16
PATCHES = 256
EPS = 1e-06


def from_everyone(shard, axis):
    size = lax.axis_size(axis)
    return lax.all_to_all(
        jnp.broadcast_to(shard[None], (size, *shard.shape)), axis, 0, 0, tiled=True
    )


def laid_out(pieces, dim):
    shape = list(pieces.shape[1:])
    shape[dim] *= pieces.shape[0]
    return jnp.moveaxis(pieces, 0, dim).reshape(shape)


def gathered_copies(shard, axis, dim):
    pieces = from_everyone(shard, axis)
    return laid_out(pieces, dim)


def split_up(shard, dim, size):
    shape = shard.shape
    pieces = shard.reshape(*shape[:dim], size, shape[dim] // size, *shape[dim + 1 :])
    return jnp.moveaxis(pieces, dim, 0)


def sum_at_owner(shard, axis, dim):
    pieces = split_up(shard, dim, lax.axis_size(axis))
    arrived = lax.all_to_all(pieces, axis, split_axis=0, concat_axis=0, tiled=True)
    return arrived.astype(jnp.float32).sum(axis=0)


def layer_norm(values, gain):
    values = values.astype(jnp.float32)
    center = values - jnp.mean(values, axis=-1, keepdims=True)
    spread = jnp.mean(center * center, axis=-1, keepdims=True)
    return (center * lax.rsqrt(spread + EPS) * gain).astype(jnp.bfloat16)


def encoder(tokens, norm_one, qkv_weight, out_weight, norm_two, up_weight, down_weight, approx):
    rows, local_width = tokens.shape
    whole = gathered_copies(tokens, "mp", 1)
    width = whole.shape[1]
    head_size = width // HEADS
    local_heads = qkv_weight.shape[2] // head_size
    scale = 1.0 / math.sqrt(head_size)
    normed = layer_norm(whole, norm_one)

    def fold_rows(source, piece):
        count = piece.shape[0]
        return jnp.dot(source, piece.reshape(count, -1), preferred_element_type=jnp.float32)

    qkv = fold_rows(normed, lax.all_gather(qkv_weight, "dp", axis=0, tiled=True))
    qkv = qkv.astype(jnp.bfloat16).reshape(rows // PATCHES, PATCHES, 3, local_heads, head_size)
    query = qkv[:, :, 0]
    keys = qkv[:, :, 1]
    values = qkv[:, :, 2]
    scores = jnp.einsum("fqhd,fkhd->fhqk", query, keys, preferred_element_type=jnp.float32) * scale
    top = jnp.max(scores, axis=-1, keepdims=True)
    expo = jnp.exp(scores - top)
    probs = (expo / jnp.sum(expo, axis=-1, keepdims=True)).astype(jnp.bfloat16)
    context = jnp.einsum("fhqk,fkhd->fqhd", probs, values, preferred_element_type=jnp.float32)
    context = context.astype(jnp.bfloat16).reshape(rows, local_heads * head_size)
    partial_attn = jnp.dot(
        context,
        lax.all_gather(out_weight, "dp", axis=1, tiled=True),
        preferred_element_type=jnp.float32,
    )
    share = sum_at_owner(partial_attn.astype(jnp.bfloat16), "mp", 1)
    middle = (tokens.astype(jnp.float32) + share).astype(jnp.bfloat16)
    middle_whole = gathered_copies(middle, "mp", 1)
    second = layer_norm(middle_whole, norm_two)
    raised = fold_rows(second, lax.all_gather(up_weight, "dp", axis=0, tiled=True))
    hidden = jax.nn.gelu(raised, approximate=approx).astype(jnp.bfloat16)
    partial_mlp = jnp.dot(
        hidden,
        lax.all_gather(down_weight, "dp", axis=1, tiled=True),
        preferred_element_type=jnp.float32,
    )
    mlp_part = sum_at_owner(partial_mlp.astype(jnp.bfloat16), "mp", 1)
    return (middle.astype(jnp.float32) + mlp_part).astype(jnp.bfloat16)


def local(
    dino_tokens,
    siglip_tokens,
    dino_norm_one,
    dino_qkv,
    dino_out,
    dino_norm_two,
    dino_up,
    dino_down,
    siglip_norm_one,
    siglip_qkv,
    siglip_out,
    siglip_norm_two,
    siglip_up,
    siglip_down,
):
    dino_result = encoder(
        dino_tokens, dino_norm_one, dino_qkv, dino_out, dino_norm_two, dino_up, dino_down, False
    )
    siglip_result = encoder(
        siglip_tokens,
        siglip_norm_one,
        siglip_qkv,
        siglip_out,
        siglip_norm_two,
        siglip_up,
        siglip_down,
        True,
    )
    return (dino_result, siglip_result)


def solution(mesh):
    in_specs = (
        P("dp", "mp"),
        P("dp", "mp"),
        P(),
        P("dp", None, "mp"),
        P("mp", "dp"),
        P(),
        P("dp", "mp"),
        P("mp", "dp"),
        P(),
        P("dp", None, "mp"),
        P("mp", "dp"),
        P(),
        P("dp", "mp"),
        P("mp", "dp"),
    )
    out_specs = (P("dp", "mp"), P("dp", "mp"))
    return jax.shard_map(local, mesh=mesh, in_specs=in_specs, out_specs=out_specs, check_vma=False)
```

profile of v0, /device:TPU:1, one launch (start us, length us, event | category | flops | bytes accessed | tf_op | source)
XLA Modules:
  0.0 1024.6 jit_solution(13799758242859776503)
XLA Ops:
  11.9 1.3 copy.43
  14.2 3.6 all-to-all-start
  17.8 11.6 %all-to-all-done = bf16[2,512,512]{1,2,0:T(8,128)(2,1)S(1)} async-done(((bf16[2,512,512]{1,2,0:T(8,128)(2,1)}), bf16[2,512,512]{1,2,0:T(8,128)(2,1)S(1)}, u32[]{:S(2)}, u32[]{:S(2)}) %all-to-all-start) | async-done | bytes 1048608 | tf_op jit(solution)/shard_map/all_to_all | solution.py:14
  30.6 3.6 all-to-all-start.4
  34.7 1.3 fusion.43
  36.1 90.8 %all-gather.12.cloned.1.call-done = bf16[1024,3,512]{2,0,1:T(8,128)(2,1)} async-done(((bf16[8,3,512]{2,0,1:T(8,128)(2,1)}), bf16[1024,3,512]{2,0,1:T(8,128)(2,1)}) %all-gather.12.cloned.1.call-update) | async-done | bytes 3145744 | tf_op jit(solution)/shard_map/all_gather | solution.py:62
  126.8 4.7 copy.44
  131.5 4.1 convolution_convert_fusion.2
  135.6 3.2 reshape.172
  138.7 3.1 fusion.101
  141.8 2.5 copy.67
  144.3 1.4 copy.68
  146.3 2.0 fusion.61
  148.3 3.2 fusion.103
  152.7 78.1 %all-gather.14.cloned.1.call-done = bf16[512,1024]{0,1:T(8,128)(2,1)} async-done(((bf16[512,8]{0,1:T(8,128)(2,1)}), bf16[512,1024]{0,1:T(8,128)(2,1)}) %all-gather.14.cloned.1.call-update) | async-done | bytes 1048592 | tf_op jit(solution)/shard_map/all_gather | solution.py:75
  230.8 2.0 convolution_convert_fusion.4
  233.9 3.6 all-to-all-start.1
  238.5 12.6 %all-to-all-done.1 = bf16[2,512,512]{2,1,0:T(8,128)(2,1)S(1)} async-done(((bf16[2,512,512]{2,1,0:T(8,128)(2,1)}), bf16[2,512,512]{2,1,0:T(8,128)(2,1)S(1)}, u32[]{:S(2)}, u32[]{:S(2)}) %all-to-all-start.1) | async-done | bytes 1048608 | tf_op jit(solution)/shard_map/all_to_all | solution.py:38
  252.8 4.0 all-to-all-start.2
  257.2 1.4 fusion.32
  258.6 91.0 %all-gather.22.cloned.1.call-done = bf16[128,9,576]{2,1,0:T(8,128)(2,1)} async-done(((bf16[1,9,576]{2,1,0:T(8,128)(2,1)}), bf16[128,9,576]{2,1,0:T(8,128)(2,1)}) %all-gather.22.cloned.1.call-update) | async-done | bytes 1327120 | tf_op jit(solution)/shard_map/all_gather | solution.py:75
  349.6 4.1 reshape.167
  353.9 118.7 %all-gather.20.cloned.1.call-done = bf16[1152,3,576]{2,1,0:T(4,128)(2,1)} async-done(((bf16[9,3,576]{2,1,0:T(4,128)(2,1)}), bf16[1152,3,576]{2,1,0:T(4,128)(2,1)}) %all-gather.20.cloned.1.call-update) | async-done | bytes 3981328 | tf_op jit(solution)/shard_map/all_gather | solution.py:62
  472.6 11.3 %copy.54 = bf16[1152,3,576]{0,2,1:T(8,128)(2,1)} copy(bf16[1152,3,576]{2,1,0:T(4,128)(2,1)} %all-gather.20.cloned.1.call-done) | data formatting | bytes 7962624 | tf_op jit(solution)/shard_map/all_gather | solution.py:62
  484.0 5.8 convolution_convert_fusion
  489.8 4.8 reshape.160
  494.6 2.6 fusion.102
  498.0 3.2 fusion.104
  503.9 1.5 copy.60
  505.3 3.7 all-to-all-start.5
  509.4 1.3 fusion.46
  510.7 13.2 %all-to-all-done.5 = bf16[2,512,576]{1,2,0:T(8,128)(2,1)S(1)} async-done(((bf16[2,512,576]{1,2,0:T(8,128)(2,1)}), bf16[2,512,576]{1,2,0:T(8,128)(2,1)S(1)}, u32[]{:S(2)}, u32[]{:S(2)}) %all-to-all-start.5) | async-done | bytes 1179680 | tf_op jit(solution)/shard_map/all_to_all | solution.py:38
  525.5 3.8 all-to-all-start.6
  529.3 63.4 %all-gather.16.cloned.1.call-done = bf16[1024,2048]{1,0:T(8,128)(2,1)} async-done(((bf16[8,2048]{1,0:T(8,128)(2,1)}), bf16[1024,2048]{1,0:T(8,128)(2,1)}) %all-gather.16.cloned.1.call-update) | async-done | bytes 4194320 | tf_op jit(solution)/shard_map/all_gather | solution.py:82
  592.7 120.0 %all-gather.18.cloned.1.call-done = bf16[2048,1024]{0,1:T(8,128)(2,1)} async-done(((bf16[2048,8]{0,1:T(8,128)(2,1)}), bf16[2048,1024]{0,1:T(8,128)(2,1)}) %all-gather.18.cloned.1.call-update) | async-done | bytes 4194320 | tf_op jit(solution)/shard_map/all_gather | solution.py:86
  712.7 17.9 %fusion.53 = bf16[512,1024]{1,0:T(8,128)(2,1)} fusion(bf16[2048,1024]{0,1:T(8,128)(2,1)} %all-gather.18.cloned.1.call-done, bf16[512,1024]{0,1:T(8,128)(2,1)} %fusion.46, bf16[1024,2048]{1,0:T(8,128)(2,1)} %all-gather.16.cloned.1.call-done), kind=kOutput, calls=%fused_computation.79 | convolution fusion | flops 4363649024 | bytes 10485760 | tf_op jit(solution)/shard_map/dot_general | solution.py:84
  730.7 2.3 copy.84
  733.0 4.5 all-to-all-start.3
  738.1 1.4 fusion.35
  739.5 103.9 %all-gather.24.cloned.1.call-done = bf16[128,9,2152]{2,1,0:T(8,128)(2,1)} async-done(((bf16[1,9,2152]{2,1,0:T(8,128)(2,1)}), bf16[128,9,2152]{2,1,0:T(8,128)(2,1)}) %all-gather.24.cloned.1.call-update) | async-done | bytes 4958224 | tf_op jit(solution)/shard_map/all_gather | solution.py:82
  843.4 9.1 reshape.169
  852.5 121.5 %all-gather.26.cloned.1.call-done = bf16[128,9,2152]{2,1,0:T(8,128)(2,1)} async-done(((bf16[1,9,2152]{2,1,0:T(8,128)(2,1)}), bf16[128,9,2152]{2,1,0:T(8,128)(2,1)}) %all-gather.26.cloned.1.call-update) | async-done | bytes 4958224 | tf_op jit(solution)/shard_map/all_gather | solution.py:86
  974.1 9.1 reshape.171
  983.2 12.2 %convolution_convert_fusion.3 = bf16[512,1152]{1,0:T(8,128)(2,1)} fusion(bf16[1152,2152]{1,0:T(8,128)(2,1)} %reshape.171, bf16[512,1152]{0,1:T(8,128)(2,1)S(1)} %copy-done.5, bf16[1152,2152]{1,0:T(8,128)(2,1)} %reshape.169), kind=kOutput, calls=%fused_computation.41 | convolution fusion | flops 5087711232 | bytes 12275712 | tf_op jit(solution)/shard_map/dot_general | solution.py:84
  995.4 2.4 copy.61
  997.8 3.6 all-to-all-start.7
  1001.4 1.5 convert_reduce_fusion.4
  1003.9 12.4 %all-to-all-done.7 = bf16[2,512,576]{1,2,0:T(8,128)(2,1)S(1)} async-done(((bf16[2,512,576]{1,2,0:T(8,128)(2,1)}), bf16[2,512,576]{1,2,0:T(8,128)(2,1)S(1)}, u32[]{:S(2)}, u32[]{:S(2)}) %all-to-all-start.7) | async-done | bytes 1179680 | tf_op jit(solution)/shard_map/all_to_all | solution.py:38
  (80 shorter events, 21.6 us)
Async XLA Ops:
  7.2 10.7 %copy-start.9 = (f32[1024]{0:T(1024)S(1)}, f32[1024]{0:T(1024)}, u32[]{:S(2)}) copy-start(f32[1024]{0:T(1024)} %param.16) | copy-start | bytes 12292
  7.2 22.3 %copy-start = (bf16[512,576]{0,1:T(8,128)(2,1)S(1)}, bf16[512,576]{0,1:T(8,128)(2,1)}, u32[]{:S(2)}) copy-start(bf16[512,576]{0,1:T(8,128)(2,1)} %param.15) | copy-start | bytes 1769476
  7.2 119.6 %all-gather.12.cloned.1.call-start = ((), (), s32[]{:S(2)}) async-start(), calls=%async_computation.8 | async-start | bytes 3170304 | tf_op jit(solution)/shard_map/all_gather | solution.py:62
  7.9 222.9 %all-gather.14.cloned.1.call-start = ((), (), s32[]{:S(2)}) async-start(), calls=%async_computation.9 | async-start | bytes 1056768 | tf_op jit(solution)/shard_map/all_gather | solution.py:75
  8.7 340.9 %all-gather.22.cloned.1.call-start = ((), (), s32[]{:S(2)}) async-start(), calls=%async_computation.13 | async-start | bytes 2641920 | tf_op jit(solution)/shard_map/all_gather | solution.py:75
  9.4 463.2 %all-gather.20.cloned.1.call-start = ((), (), s32[]{:S(2)}) async-start(), calls=%async_computation.12 | async-start | bytes 5944320 | tf_op jit(solution)/shard_map/all_gather | solution.py:62
  10.0 582.7 %all-gather.16.cloned.1.call-start = ((), (), s32[]{:S(2)}) async-start(), calls=%async_computation.10 | async-start | bytes 4227072 | tf_op jit(solution)/shard_map/all_gather | solution.py:82
  10.6 702.2 %all-gather.18.cloned.1.call-start = ((), (), s32[]{:S(2)}) async-start(), calls=%async_computation.11 | async-start | bytes 4227072 | tf_op jit(solution)/shard_map/all_gather | solution.py:86
  11.1 832.3 %all-gather.24.cloned.1.call-start = ((), (), s32[]{:S(2)}) async-start(), calls=%async_computation.14 | async-start | bytes 8982528 | tf_op jit(solution)/shard_map/all_gather | solution.py:82
  14.2 15.2 %all-to-all-start = ((bf16[2,512,512]{1,2,0:T(8,128)(2,1)}), bf16[2,512,512]{1,2,0:T(8,128)(2,1)S(1)}, u32[]{:S(2)}, u32[]{:S(2)}) async-start(bf16[2,512,512]{1,2,0:T(8,128)(2,1)} %broadcast_in_dim.8), calls=%async_computation | async-start | bytes 2097152 | tf_op jit(solution)/shard_map/all_to_all | solution.py:14
  30.6 203.3 %all-to-all-start.4 = ((bf16[2,512,576]{1,2,0:T(8,128)(2,1)}), bf16[2,512,576]{1,2,0:T(8,128)(2,1)S(1)}, u32[]{:S(2)}, u32[]{:S(2)}) async-start(bf16[2,512,576]{1,2,0:T(8,128)(2,1)} %broadcast_in_dim.10), calls=%async_computation.4 | async-start | bytes 2359296 | tf_op jit(solution)/shard_map/all_to_all | solution.py:14
  152.6 85.7 %copy-start.7 = (f32[1152]{0:T(1024)S(1)}, f32[1152]{0:T(1024)}, u32[]{:S(2)}) copy-start(f32[1152]{0:T(1024)} %param.22) | copy-start | bytes 13828
  232.8 18.5 %copy-start.2 = (bf16[512,512]{1,0:T(8,128)(2,1)S(1)}, bf16[512,512]{1,0:T(8,128)(2,1)}, u32[]{:S(2)}) copy-start(bf16[512,512]{1,0:T(8,128)(2,1)} %param.14) | copy-start | bytes 1572868
  233.9 17.2 %all-to-all-start.1 = ((bf16[2,512,512]{2,1,0:T(8,128)(2,1)}), bf16[2,512,512]{2,1,0:T(8,128)(2,1)S(1)}, u32[]{:S(2)}, u32[]{:S(2)}) async-start(bf16[2,512,512]{2,1,0:T(8,128)(2,1)} %bitcast.102), calls=%async_computation.1 | async-start | bytes 2097152 | tf_op jit(solution)/shard_map/all_to_all | solution.py:38
  237.5 736.6 %all-gather.26.cloned.1.call-start = ((), (), s32[]{:S(2)}) async-start(), calls=%async_computation.15 | async-start | bytes 8982528 | tf_op jit(solution)/shard_map/all_gather | solution.py:86
  252.8 100.9 %all-to-all-start.2 = ((bf16[2,512,512]{1,2,0:T(8,128)(2,1)}), bf16[2,512,512]{1,2,0:T(8,128)(2,1)S(1)}, u32[]{:S(2)}, u32[]{:S(2)}) async-start(bf16[2,512,512]{1,2,0:T(8,128)(2,1)} %broadcast_in_dim.9), calls=%async_computation.2 | async-start | bytes 2097152 | tf_op jit(solution)/shard_map/all_to_all | solution.py:14
  353.9 130.0 %copy-start.4 = (bf16[2,512,576]{1,2,0:T(8,128)(2,1)S(1)}, bf16[2,512,576]{1,2,0:T(8,128)(2,1)}, u32[]{:S(2)}) copy-start(bf16[2,512,576]{1,2,0:T(8,128)(2,1)} %fusion.32) | copy-start | bytes 3538948
  501.2 1.4 copy-start.3
  502.6 6.8 copy-start.8
  505.3 18.8 %copy-start.1 = (bf16[512,576]{0,1:T(8,128)(2,1)S(1)}, bf16[512,576]{0,1:T(8,128)(2,1)}, u32[]{:S(2)}) copy-start(bf16[512,576]{0,1:T(8,128)(2,1)} %param.15) | copy-start | bytes 1769476
  505.3 18.6 %all-to-all-start.5 = ((bf16[2,512,576]{1,2,0:T(8,128)(2,1)}), bf16[2,512,576]{1,2,0:T(8,128)(2,1)S(1)}, u32[]{:S(2)}, u32[]{:S(2)}) async-start(bf16[2,512,576]{1,2,0:T(8,128)(2,1)} %bitcast.21), calls=%async_computation.5 | async-start | bytes 2359296 | tf_op jit(solution)/shard_map/all_to_all | solution.py:38
  525.5 207.5 %all-to-all-start.6 = ((bf16[2,512,576]{1,2,0:T(8,128)(2,1)}), bf16[2,512,576]{1,2,0:T(8,128)(2,1)S(1)}, u32[]{:S(2)}, u32[]{:S(2)}) async-start(bf16[2,512,576]{1,2,0:T(8,128)(2,1)} %broadcast_in_dim.11), calls=%async_computation.6 | async-start | bytes 2359296 | tf_op jit(solution)/shard_map/all_to_all | solution.py:14
  730.7 7.4 copy-start.6
  733.0 264.8 %all-to-all-start.3 = ((bf16[2,512,512]{2,1,0:T(8,128)(2,1)}), bf16[2,512,512]{2,1,0:T(8,128)(2,1)}, u32[]{:S(2)}, u32[]{:S(2)}) async-start(bf16[2,512,512]{2,1,0:T(8,128)(2,1)} %bitcast.103), calls=%async_computation.3 | async-start | bytes 2097152 | tf_op jit(solution)/shard_map/all_to_all | solution.py:38
  852.5 130.7 %copy-start.5 = (bf16[512,1152]{0,1:T(8,128)(2,1)S(1)}, bf16[512,1152]{0,1:T(8,128)(2,1)}, u32[]{:S(2)}) copy-start(bf16[512,1152]{0,1:T(8,128)(2,1)} %fusion.35) | copy-start | bytes 3538948
  997.8 18.4 %all-to-all-start.7 = ((bf16[2,512,576]{1,2,0:T(8,128)(2,1)}), bf16[2,512,576]{1,2,0:T(8,128)(2,1)S(1)}, u32[]{:S(2)}, u32[]{:S(2)}) async-start(bf16[2,512,576]{1,2,0:T(8,128)(2,1)} %bitcast.28), calls=%async_computation.7 | async-start | bytes 2359296 | tf_op jit(solution)/shard_map/all_to_all | solution.py:38
Sparse Core Ops, SparseCore 0:
  11.8 114.9 all-gather.11
  130.6 100.1 all-gather.13
  234.4 115.1 all-gather.21
  353.1 119.4 all-gather.19
  476.0 116.5 all-gather.15
  596.1 116.5 all-gather.17
  716.3 127.0 all-gather.23
  847.0 127.0 all-gather.25
where the time goes:
time: 1030 us; the launch traced here: 1020 us
  waiting for transfers between devices  842 us (82%)
  local copies, waits for them, and re-layouts  71.3 us (7%)
  matrix products  46.9 us (5%)
  starting transfers between devices  30.7 us (3%)
  other arithmetic  18.8 us (2%)
  between operations  14.7 us (1%)
    all_gather x2, waiting for transfers between devices, encoder(): lax.all_gather(down_weight, 'dp', axis=1, tiled=True)  242 us
    all_gather x2, waiting for transfers between devices, encoder(): lax.all_gather(qkv_weight, 'dp', axis=0, tiled=True)  209 us
    all_gather x2, waiting for transfers between devices, encoder(): lax.all_gather(out_weight, 'dp', axis=1, tiled=True)  169 us
    all_gather x2, waiting for transfers between devices, encoder(): lax.all_gather(up_weight, 'dp', axis=0, tiled=True)  167 us
    all_to_all x4, waiting for transfers between devices, sum_at_owner(): lax.all_to_all(pieces, axis, split_axis=0, concat_axis=0, tiled=True)  38.1 us
    dot_general x2, matrix products, encoder(): jnp.dot(hidden, lax.all_gather(down_weight, 'dp', axis=1, tiled=True), pr...  30.1 us
    unnamed x29, local copies, waits for them, and re-layouts  28.5 us
  transfers between devices with their start and end apart: 16, of which 12 were waited for; matrix products, arithmetic and copies ran while one was open for 13% of the time, Pallas kernels for 0%

commit v1 on v0

--- a/solution.py
+++ b/solution.py
@@ -7,6 +7,11 @@
 HEADS = 16
 PATCHES = 256
 EPS = 1e-06
+
+
+def exchange_gather(x, axis, dim):
+    repeated = jnp.stack([x] * lax.axis_size(axis))
+    return jnp.concatenate(lax.all_to_all(repeated, axis, 0, 0), axis=dim)
 
 
 def from_everyone(shard, axis):
@@ -59,7 +64,7 @@
         count = piece.shape[0]
         return jnp.dot(source, piece.reshape(count, -1), preferred_element_type=jnp.float32)
 
-    qkv = fold_rows(normed, lax.all_gather(qkv_weight, "dp", axis=0, tiled=True))
+    qkv = fold_rows(normed, exchange_gather(qkv_weight, "dp", 0))
     qkv = qkv.astype(jnp.bfloat16).reshape(rows // PATCHES, PATCHES, 3, local_heads, head_size)
     query = qkv[:, :, 0]
     keys = qkv[:, :, 1]

time: 1030 us -> 830 us (0.81)
  waiting for transfers between devices: 842 us -> 583 us
  blocking collectives: 0 us -> 41 us
  starting transfers between devices: 30.7 us -> 52.3 us
    all_gather x2 -> x0, waiting for transfers between devices: 209 us -> none  [encoder(): lax.all_gather(qkv_weight, 'dp', axis=0, tiled=True)]
    all_to_all x0 -> x2, waiting for transfers between devices: none -> 159 us  [exchange_gather(): return jnp.concatenate(lax.all_to_all(repeated, axis, 0, 0), axis=dim)]
    all_gather x2, waiting for transfers between devices: 169 us -> 50.6 us  [encoder(): lax.all_gather(out_weight, 'dp', axis=1, tiled=True)]
    all_gather x2, waiting for transfers between devices: 167 us -> 107 us  [encoder(): lax.all_gather(up_weight, 'dp', axis=0, tiled=True)]
    all_to_all x0 -> x3, blocking collectives: none -> 41 us  [the longest x2 26.3 us: from_everyone(): lax.all_to_all(jnp.broadcast_to(shard[None], (size, *shard.shape)), axis,...]
    all_to_all x0 -> x2, starting transfers between devices: none -> 33.5 us  [exchange_gather(): return jnp.concatenate(lax.all_to_all(repeated, axis, 0, 0), axis=dim)]
    another operation x0 -> x3, local copies, waits for them, and re-layouts: none -> 18.2 us  [the longest x1 12.4 us: fold_rows(): piece.reshape(count, -1)]
    all_gather x2 -> x0, local copies, waits for them, and re-layouts: 16 us -> none  [encoder(): lax.all_gather(qkv_weight, 'dp', axis=0, tiled=True)]
  transfers between devices with their start and end apart: 16 -> 13, of which waited for: 12 -> 9; matrix products, arithmetic and copies ran while one was open for 13% -> 16% of each run, Pallas kernels for 0% -> 0%
where the time goes in v1:
time: 830 us; the launch traced here: 820 us
  waiting for transfers between devices  583 us (70%)
  local copies, waits for them, and re-layouts  67.3 us (8%)
  starting transfers between devices  52.3 us (6%)
  matrix products  45.6 us (5%)
  blocking collectives  41 us (5%)
  other arithmetic  16.4 us (2%)
  between operations  14.7 us (2%)
    all_gather x2, waiting for transfers between devices, encoder(): lax.all_gather(down_weight, 'dp', axis=1, tiled=True)  227 us
    all_to_all x2, waiting for transfers between devices, exchange_gather(): return jnp.concatenate(lax.all_to_all(repeated, axis, 0, 0), axis=dim)  159 us
    all_gather x2, waiting for transfers between devices, encoder(): lax.all_gather(up_weight, 'dp', axis=0, tiled=True)  107 us
    all_gather x2, waiting for transfers between devices, encoder(): lax.all_gather(out_weight, 'dp', axis=1, tiled=True)  50.6 us
    all_to_all x2, starting transfers between devices, exchange_gather(): return jnp.concatenate(lax.all_to_all(repeated, axis, 0, 0), axis=dim)  33.5 us
    unnamed x33, local copies, waits for them, and re-layouts  29.2 us
    dot_general x2, matrix products, encoder(): jnp.dot(hidden, lax.all_gather(down_weight, 'dp', axis=1, tiled=True), pr...  29.1 us
    all_to_all x2, blocking collectives, from_everyone(): lax.all_to_all(jnp.broadcast_to(shard[None], (size, *shard.shape)), axis,...  26.3 us
  transfers between devices with their start and end apart: 13, of which 9 were waited for; matrix products, arithmetic and copies ran while one was open for 16% of the time, Pallas kernels for 0%

profile of v1, /device:TPU:1, one launch (start us, length us, event | category | flops | bytes accessed | tf_op | source)
XLA Modules:
  0.0 820.3 jit_solution(4557272339010694307)
XLA Ops:
  10.0 1.3 copy.43
  11.3 14.2 %all_to_all.50 = bf16[2,512,512]{1,2,0:T(8,128)(2,1)S(1)} all-to-all(bf16[2,512,512]{1,2,0:T(8,128)(2,1)S(1)} %broadcast_in_dim.8), channel_id=1, replica_groups=mesh['dp'=128,'mp'=2] {'mp'}, dimensions={0} | all-to-all | bytes 2097152 | tf_op jit(solution)/shard_map/all_to_all | solution.py:19
  25.5 1.9 stack.4
  27.4 18.9 %all-to-all-start.1 = ((bf16[128,8,3,512]{3,1,2,0:T(8,128)(2,1)}), bf16[128,8,3,512]{3,1,2,0:T(8,128)(2,1)}, u32[]{:S(2)}, u32[]{:S(2)}) async-start(bf16[128,8,3,512]{3,1,2,0:T(8,128)(2,1)} %stack.4), calls=%async_computation.1 | async-start | bytes 6291456 | tf_op jit(solution)/shard_map/all_to_all | solution.py:14
  47.8 75.3 %all-to-all-done.1 = bf16[128,8,3,512]{3,1,2,0:T(8,128)(2,1)} async-done(((bf16[128,8,3,512]{3,1,2,0:T(8,128)(2,1)}), bf16[128,8,3,512]{3,1,2,0:T(8,128)(2,1)}, u32[]{:S(2)}, u32[]{:S(2)}) %all-to-all-start.1) | async-done | bytes 3145760 | tf_op jit(solution)/shard_map/all_to_all | solution.py:14
  123.1 4.9 convolution_convert_fusion.2
  128.0 4.0 reshape.168
  132.0 1.9 fusion.101
  133.9 1.7 copy.65
  135.6 1.7 copy.66
  137.3 1.7 copy.64
  139.8 3.2 fusion.103
  144.2 2.0 convolution_convert_fusion.4
  146.3 14.7 %all_to_all.51 = bf16[2,512,512]{2,1,0:T(8,128)(2,1)S(1)} all-to-all(bf16[2,512,512]{2,1,0:T(8,128)(2,1)S(1)} %bitcast.103), channel_id=1, replica_groups=mesh['dp'=128,'mp'=2] {'mp'}, dimensions={0} | all-to-all | bytes 2097152 | tf_op jit(solution)/shard_map/all_to_all | solution.py:43
  161.1 1.1 broadcast_in_dim.10
  162.2 3.6 all-to-all-start.5
  166.4 12.1 %all-to-all-done.5 = bf16[2,512,576]{1,2,0:T(8,128)(2,1)S(1)} async-done(((bf16[2,512,576]{1,2,0:T(8,128)(2,1)}), bf16[2,512,576]{1,2,0:T(8,128)(2,1)S(1)}, u32[]{:S(2)}, u32[]{:S(2)}) %all-to-all-start.5) | async-done | bytes 1179680 | tf_op jit(solution)/shard_map/all_to_all | solution.py:19
  178.5 12.1 %all_to_all.52 = bf16[2,512,512]{1,2,0:T(8,128)(2,1)S(1)} all-to-all(bf16[2,512,512]{1,2,0:T(8,128)(2,1)S(1)} %broadcast_in_dim.9), channel_id=1, replica_groups=mesh['dp'=128,'mp'=2] {'mp'}, dimensions={0} | all-to-all | bytes 2097152 | tf_op jit(solution)/shard_map/all_to_all | solution.py:19
  190.7 4.0 stack.5
  194.7 14.6 %all-to-all-start.6 = ((bf16[128,9,3,576]{3,2,1,0:T(4,128)(2,1)}), bf16[128,9,3,576]{3,2,1,0:T(4,128)(2,1)}, u32[]{:S(2)}, u32[]{:S(2)}) async-start(bf16[128,9,3,576]{3,2,1,0:T(4,128)(2,1)} %stack.5), calls=%async_computation.6 | async-start | bytes 11796480 | tf_op jit(solution)/shard_map/all_to_all | solution.py:14
  210.6 1.4 fusion.32
  211.9 50.6 %all-gather.16.cloned.1.call-done = bf16[128,9,576]{2,1,0:T(8,128)(2,1)} async-done(((bf16[1,9,576]{2,1,0:T(8,128)(2,1)}), bf16[128,9,576]{2,1,0:T(8,128)(2,1)}) %all-gather.16.cloned.1.call-update) | async-done | bytes 1327120 | tf_op jit(solution)/shard_map/all_gather | solution.py:80
  262.5 4.1 reshape.163
  266.8 83.5 %all-to-all-done.6 = bf16[128,9,3,576]{3,2,1,0:T(4,128)(2,1)} async-done(((bf16[128,9,3,576]{3,2,1,0:T(4,128)(2,1)}), bf16[128,9,3,576]{3,2,1,0:T(4,128)(2,1)}, u32[]{:S(2)}, u32[]{:S(2)}) %all-to-all-start.6) | async-done | bytes 3981344 | tf_op jit(solution)/shard_map/all_to_all | solution.py:14
  350.3 12.4 %reshape_reshape.7 = bf16[1152,1728]{1,0:T(8,128)(2,1)} reshape(bf16[128,9,3,576]{3,2,1,0:T(4,128)(2,1)} %all-to-all-done.6) | data formatting | bytes 7962624 | tf_op jit(solution)/shard_map/reshape;reshape | solution.py:65
  362.6 6.0 convolution_convert_fusion.1
  368.6 3.9 reshape.156
  372.5 1.2 fusion.102
  374.5 3.2 fusion.104
  379.1 1.2 convolution_convert_fusion
  380.3 1.4 copy.58
  381.8 3.7 all-to-all-start.7
  385.9 1.3 fusion.46
  387.2 10.7 %all-to-all-done.7 = bf16[2,512,576]{1,2,0:T(8,128)(2,1)S(1)} async-done(((bf16[2,512,576]{1,2,0:T(8,128)(2,1)}), bf16[2,512,576]{1,2,0:T(8,128)(2,1)S(1)}, u32[]{:S(2)}, u32[]{:S(2)}) %all-to-all-start.7) | async-done | bytes 1179680 | tf_op jit(solution)/shard_map/all_to_all | solution.py:43
  398.4 1.1 broadcast_in_dim.11
  399.5 4.0 all-to-all-start.8
  403.6 105.2 %all-gather.14.cloned.1.call-done = bf16[2048,1024]{0,1:T(8,128)(2,1)} async-done(((bf16[2048,8]{0,1:T(8,128)(2,1)}), bf16[2048,1024]{0,1:T(8,128)(2,1)}) %all-gather.14.cloned.1.call-update) | async-done | bytes 4194320 | tf_op jit(solution)/shard_map/all_gather | solution.py:91
  508.8 16.9 %fusion.53 = bf16[512,1024]{1,0:T(8,128)(2,1)S(1)} fusion(bf16[2048,1024]{0,1:T(8,128)(2,1)} %all-gather.14.cloned.1.call-done, bf16[512,1024]{0,1:T(8,128)(2,1)} %fusion.46, bf16[1024,2048]{1,0:T(8,128)(2,1)} %all-gather.12.cloned.1.call-done), kind=kOutput, calls=%fused_computation.79 | convolution fusion | flops 4363649024 | bytes 10485760 | tf_op jit(solution)/shard_map/dot_general | solution.py:89
  526.8 3.6 all-to-all-start.4
  531.0 1.4 fusion.35
  532.4 106.9 %all-gather.18.cloned.1.call-done = bf16[128,9,2152]{2,1,0:T(8,128)(2,1)} async-done(((bf16[1,9,2152]{2,1,0:T(8,128)(2,1)}), bf16[128,9,2152]{2,1,0:T(8,128)(2,1)}) %all-gather.18.cloned.1.call-update) | async-done | bytes 4958224 | tf_op jit(solution)/shard_map/all_gather | solution.py:87
  639.3 9.2 %reshape.165 = bf16[1152,2152]{1,0:T(8,128)(2,1)} reshape(bf16[128,9,2152]{2,1,0:T(8,128)(2,1)} %all-gather.18.cloned.1.call-done) | data formatting | bytes 9916416
  648.5 121.3 %all-gather.20.cloned.1.call-done = bf16[128,9,2152]{2,1,0:T(8,128)(2,1)} async-done(((bf16[1,9,2152]{2,1,0:T(8,128)(2,1)}), bf16[128,9,2152]{2,1,0:T(8,128)(2,1)}) %all-gather.20.cloned.1.call-update) | async-done | bytes 4958224 | tf_op jit(solution)/shard_map/all_gather | solution.py:91
  769.8 9.1 %reshape.167 = bf16[1152,2152]{1,0:T(8,128)(2,1)} reshape(bf16[128,9,2152]{2,1,0:T(8,128)(2,1)} %all-gather.20.cloned.1.call-done) | data formatting | bytes 9916416
  779.0 12.2 %convolution_convert_fusion.3 = bf16[512,1152]{1,0:T(8,128)(2,1)} fusion(bf16[1152,2152]{1,0:T(8,128)(2,1)} %reshape.167, bf16[512,1152]{0,1:T(8,128)(2,1)S(1)} %copy-done.5, bf16[1152,2152]{1,0:T(8,128)(2,1)} %reshape.165), kind=kOutput, calls=%fused_computation.41 | convolution fusion | flops 5087711232 | bytes 12275712 | tf_op jit(solution)/shard_map/dot_general | solution.py:89
  791.1 2.4 copy.59
  793.5 3.6 all-to-all-start.9
  798.3 13.7 %all-to-all-done.9 = bf16[2,512,576]{1,2,0:T(8,128)(2,1)S(1)} async-done(((bf16[2,512,576]{1,2,0:T(8,128)(2,1)}), bf16[2,512,576]{1,2,0:T(8,128)(2,1)S(1)}, u32[]{:S(2)}, u32[]{:S(2)}) %all-to-all-start.9) | async-done | bytes 1179680 | tf_op jit(solution)/shard_map/all_to_all | solution.py:43
  (80 shorter events, 15.4 us)
Async XLA Ops:
  7.2 18.4 %copy-start.7 = (bf16[8,3,512]{2,0,1:T(8,128)(2,1)S(1)}, bf16[8,3,512]{2,0,1:T(8,128)(2,1)}, u32[]{:S(2)}) copy-start(bf16[8,3,512]{2,0,1:T(8,128)(2,1)} %param.17) | copy-start | bytes 73732
  7.2 137.0 %all-gather.10.cloned.1.call-start = ((), (), s32[]{:S(2)}) async-start(), calls=%async_computation.10 | async-start | bytes 1056768 | tf_op jit(solution)/shard_map/all_gather | solution.py:80
  7.9 254.6 %all-gather.16.cloned.1.call-start = ((), (), s32[]{:S(2)}) async-start(), calls=%async_computation.13 | async-start | bytes 2641920 | tf_op jit(solution)/shard_map/all_gather | solution.py:80
  8.7 394.9 %all-gather.12.cloned.1.call-start = ((), (), s32[]{:S(2)}) async-start(), calls=%async_computation.11 | async-start | bytes 4227072 | tf_op jit(solution)/shard_map/all_gather | solution.py:87
  9.4 499.4 %all-gather.14.cloned.1.call-start = ((), (), s32[]{:S(2)}) async-start(), calls=%async_computation.12 | async-start | bytes 4227072 | tf_op jit(solution)/shard_map/all_gather | solution.py:91
  25.5 21.4 %copy-start.11 = (f32[1024]{0:T(1024)S(1)}, f32[1024]{0:T(1024)}, u32[]{:S(2)}) copy-start(f32[1024]{0:T(1024)} %param.16) | copy-start | bytes 12292
  27.4 95.7 %all-to-all-start.1 = ((bf16[128,8,3,512]{3,1,2,0:T(8,128)(2,1)}), bf16[128,8,3,512]{3,1,2,0:T(8,128)(2,1)}, u32[]{:S(2)}, u32[]{:S(2)}) async-start(bf16[128,8,3,512]{3,1,2,0:T(8,128)(2,1)} %stack.4), calls=%async_computation.1 | async-start | bytes 6291456 | tf_op jit(solution)/shard_map/all_to_all | solution.py:14
  46.3 593.0 %all-gather.18.cloned.1.call-start = ((), (), s32[]{:S(2)}) async-start(), calls=%async_computation.14 | async-start | bytes 8982528 | tf_op jit(solution)/shard_map/all_gather | solution.py:87
  144.1 17.0 %copy-start = (bf16[512,576]{0,1:T(8,128)(2,1)S(1)}, bf16[512,576]{0,1:T(8,128)(2,1)}, u32[]{:S(2)}) copy-start(bf16[512,576]{0,1:T(8,128)(2,1)} %param.15) | copy-start | bytes 1769476
  146.3 19.7 %copy-start.2 = (bf16[512,512]{1,0:T(8,128)(2,1)S(1)}, bf16[512,512]{1,0:T(8,128)(2,1)}, u32[]{:S(2)}) copy-start(bf16[512,512]{1,0:T(8,128)(2,1)} %param.14) | copy-start | bytes 1572868
  162.2 16.3 %all-to-all-start.5 = ((bf16[2,512,576]{1,2,0:T(8,128)(2,1)}), bf16[2,512,576]{1,2,0:T(8,128)(2,1)S(1)}, u32[]{:S(2)}, u32[]{:S(2)}) async-start(bf16[2,512,576]{1,2,0:T(8,128)(2,1)} %broadcast_in_dim.10), calls=%async_computation.5 | async-start | bytes 2359296 | tf_op jit(solution)/shard_map/all_to_all | solution.py:19
  165.8 24.8 %copy-start.6 = (bf16[9,3,576]{2,1,0:T(4,128)(2,1)S(1)}, bf16[9,3,576]{2,1,0:T(4,128)(2,1)}, u32[]{:S(2)}) copy-start(bf16[9,3,576]{2,1,0:T(4,128)(2,1)} %param.23) | copy-start | bytes 93316
  194.7 15.2 %copy-start.9 = (f32[1152]{0:T(1024)S(1)}, f32[1152]{0:T(1024)}, u32[]{:S(2)}) copy-start(f32[1152]{0:T(1024)} %param.22) | copy-start | bytes 13828
  194.7 155.6 %all-to-all-start.6 = ((bf16[128,9,3,576]{3,2,1,0:T(4,128)(2,1)}), bf16[128,9,3,576]{3,2,1,0:T(4,128)(2,1)}, u32[]{:S(2)}, u32[]{:S(2)}) async-start(bf16[128,9,3,576]{3,2,1,0:T(4,128)(2,1)} %stack.5), calls=%async_computation.6 | async-start | bytes 11796480 | tf_op jit(solution)/shard_map/all_to_all | solution.py:14
  209.3 560.5 %all-gather.20.cloned.1.call-start = ((), (), s32[]{:S(2)}) async-start(), calls=%async_computation.15 | async-start | bytes 8982528 | tf_op jit(solution)/shard_map/all_gather | solution.py:91
  266.8 95.8 %copy-start.4 = (bf16[2,512,576]{1,2,0:T(8,128)(2,1)S(1)}, bf16[2,512,576]{1,2,0:T(8,128)(2,1)}, u32[]{:S(2)}) copy-start(bf16[2,512,576]{1,2,0:T(8,128)(2,1)} %fusion.32) | copy-start | bytes 3538948
  377.8 1.4 copy-start.3
  379.1 6.8 copy-start.10
  381.8 16.3 %copy-start.1 = (bf16[512,576]{0,1:T(8,128)(2,1)S(1)}, bf16[512,576]{0,1:T(8,128)(2,1)}, u32[]{:S(2)}) copy-start(bf16[512,576]{0,1:T(8,128)(2,1)} %param.15) | copy-start | bytes 1769476
  381.8 16.1 %all-to-all-start.7 = ((bf16[2,512,576]{1,2,0:T(8,128)(2,1)}), bf16[2,512,576]{1,2,0:T(8,128)(2,1)S(1)}, u32[]{:S(2)}, u32[]{:S(2)}) async-start(bf16[2,512,576]{1,2,0:T(8,128)(2,1)} %bitcast.20), calls=%async_computation.7 | async-start | bytes 2359296 | tf_op jit(solution)/shard_map/all_to_all | solution.py:43
  399.5 127.3 %all-to-all-start.8 = ((bf16[2,512,576]{1,2,0:T(8,128)(2,1)}), bf16[2,512,576]{1,2,0:T(8,128)(2,1)S(1)}, u32[]{:S(2)}, u32[]{:S(2)}) async-start(bf16[2,512,576]{1,2,0:T(8,128)(2,1)} %broadcast_in_dim.11), calls=%async_computation.8 | async-start | bytes 2359296 | tf_op jit(solution)/shard_map/all_to_all | solution.py:19
  525.7 5.3 copy-start.8
  526.8 266.8 %all-to-all-start.4 = ((bf16[2,512,512]{2,1,0:T(8,128)(2,1)}), bf16[2,512,512]{2,1,0:T(8,128)(2,1)S(1)}, u32[]{:S(2)}, u32[]{:S(2)}) async-start(bf16[2,512,512]{2,1,0:T(8,128)(2,1)} %bitcast.102), calls=%async_computation.4 | async-start | bytes 2097152 | tf_op jit(solution)/shard_map/all_to_all | solution.py:43
  648.5 130.5 %copy-start.5 = (bf16[512,1152]{0,1:T(8,128)(2,1)S(1)}, bf16[512,1152]{0,1:T(8,128)(2,1)}, u32[]{:S(2)}) copy-start(bf16[512,1152]{0,1:T(8,128)(2,1)} %fusion.35) | copy-start | bytes 3538948
  793.5 18.4 %all-to-all-start.9 = ((bf16[2,512,576]{1,2,0:T(8,128)(2,1)}), bf16[2,512,576]{1,2,0:T(8,128)(2,1)S(1)}, u32[]{:S(2)}, u32[]{:S(2)}) async-start(bf16[2,512,576]{1,2,0:T(8,128)(2,1)} %bitcast.27), calls=%async_computation.9 | async-start | bytes 2359296 | tf_op jit(solution)/shard_map/all_to_all | solution.py:43
Sparse Core Ops, SparseCore 0:
  11.7 116.2 all-gather.9
  131.6 130.8 all-gather.15
  266.1 122.5 all-gather.11
  392.2 116.5 all-gather.13
  512.2 127.0 all-gather.17
  642.8 127.0 all-gather.19
